TPU v7x, 256 devices: a whole 4x4x8 slice. The times are simulated.
256 devices in a mesh: section: 4 (over y_hi, core), dp: 64 (over y_lo, x, z).
Axes of the slice: x: 4, y: 4 (y_hi: 2, y_lo: 2; y = y_hi * 2 + y_lo), z: 8, core: 2. Of those that a mesh axis runs over, the one named last changes fastest.
Arguments:
- section_inputs: bfloat16 [4, 2, 8192, 1024], P('section', None, 'dp'), may hold values from -16 to 16
- gain: float32 [4, 1024], P('section'), may hold values from 0.25 to 1.75
- w_gate: bfloat16 [4, 1024, 1536], P('section'), may hold values from -0.1875 to 0.1875
- w_up: bfloat16 [4, 1024, 1536], P('section'), may hold values from -0.1875 to 0.1875
- w_out: bfloat16 [4, 1024, 1536], P('section'), may hold values from -0.15625 to 0.15625
- out_grad: bfloat16 [2, 8192, 1024], P(None, 'dp'), may hold values from -16 to 16
Outputs:
- grad_w_gate: float32 [4, 1024, 1536], P('section', 'dp')
- grad_w_up: float32 [4, 1024, 1536], P('section', 'dp')
- grad_w_out: float32 [4, 1024, 1536], P('section', 'dp')
- grad_gain: float32 [4, 1024], P('section', 'dp')
- input_grads: bfloat16 [4, 2, 8192, 1024], P('section', None, 'dp')
All inputs are finite; a program needn't handle non-finite values.
Results may differ from a plain program's by a relative error of at most 0.014.
Values may be sent and summed in bfloat16 or wider, within the bound.
No kernel may reach another device: no remote copies, remote signals or barrier semaphores. Data moves between devices by JAX's collectives and lax.ppermute only.
A program may use at most 128 MiB of HBM per device.

v0:
```python
import jax
import jax.numpy as jnp
from jax import lax
from jax.sharding import Mesh
from jax.sharding import PartitionSpec as P

DP = ("dp_0", "dp_1", "dp_2")


C_GELU = 0.7978845608028654
EPSILON = 1e-06


def from_behind(value, axis, steps):
    count = lax.axis_size(axis)
    leading, last = (max(0, -steps), min(count, count - steps))
    return lax.ppermute(value, axis, [(source, source + steps) for source in range(leading, last)])


def reduced_to_own(blocks, axes, order):
    shape = [lax.axis_size(a) for a in axes]
    blocks = blocks.reshape(*shape, *blocks.shape[1:])
    blocks = blocks.transpose(*order, *range(len(axes), blocks.ndim))
    blocks = blocks.reshape(-1, *blocks.shape[len(axes) :])
    for k in order:
        blocks = lax.psum_scatter(blocks, axes[k], scatter_dimension=0, tiled=True)
    return blocks[0]


def split_up(x, dim, peers):
    shape = x.shape
    blocks = x.reshape(*shape[:dim], peers, shape[dim] // peers, *shape[dim + 1 :])
    return jnp.moveaxis(blocks, dim, 0)


def scatter_axes(x, axes, order, dim):
    peers = lax.axis_size(axes)
    return reduced_to_own(split_up(x, dim, peers), axes, order)


def sum_at_owner(x, axis, dim):
    peers = lax.axis_size(axis)
    blocks = lax.all_to_all(split_up(x, dim, peers), axis, 0, 0, tiled=True)
    return jnp.sum(blocks, axis=0)


def gelu_parts(pre_act):
    cubic = 0.044715 * pre_act * pre_act * pre_act
    tangent = jnp.tanh(C_GELU * (pre_act + cubic))
    gelu_value = 0.5 * pre_act * (1.0 + tangent)
    gelu_slope = 0.5 * (1.0 + tangent) + 0.5 * pre_act * (1.0 - tangent * tangent) * C_GELU * (
        1.0 + 3.0 * 0.044715 * pre_act * pre_act
    )
    return (gelu_value, gelu_slope)


def section_back(inputs_row, incoming, gain_row, w_gate_mat, w_up_mat, w_out_mat):
    inputs_float = inputs_row.astype(jnp.float32)
    inverse_rms = lax.rsqrt(jnp.mean(inputs_float * inputs_float, axis=-1, keepdims=True) + EPSILON)
    normed = (inputs_float * inverse_rms * gain_row).astype(jnp.bfloat16)
    gate_pre = jnp.dot(normed, w_gate_mat, preferred_element_type=jnp.float32)
    up_pre = jnp.dot(normed, w_up_mat, preferred_element_type=jnp.float32)
    gelu_value, gelu_slope = gelu_parts(gate_pre)
    hidden_act = (gelu_value * up_pre).astype(jnp.bfloat16)
    act_grad = jnp.dot(incoming, w_out_mat, preferred_element_type=jnp.float32)
    gate_grad = (act_grad * up_pre * gelu_slope).astype(jnp.bfloat16)
    up_grad = (act_grad * gelu_value).astype(jnp.bfloat16)
    transpose_dims = (((1,), (1,)), ((), ()))
    normed_grad = lax.dot_general(
        gate_grad, w_gate_mat, transpose_dims, preferred_element_type=jnp.float32
    )
    normed_grad = normed_grad + lax.dot_general(
        up_grad, w_up_mat, transpose_dims, preferred_element_type=jnp.float32
    )
    gain_term = jnp.sum(normed_grad * inputs_float * inverse_rms, axis=0)
    scaled_grad = normed_grad * gain_row
    input_grad = inverse_rms * scaled_grad - inputs_float * inverse_rms**3 * jnp.mean(
        scaled_grad * inputs_float, axis=-1, keepdims=True
    )
    passed = (incoming.astype(jnp.float32) + input_grad).astype(jnp.bfloat16)
    return (passed, hidden_act, gate_grad, up_grad, normed, gain_term)


def local(section_inputs, gain, w_gate, w_up, w_out, out_grad):
    section_count = lax.axis_size("section")
    position = lax.axis_index("section")
    inputs_here = section_inputs[0]
    gain_row = gain[0]
    w_gate_mat = w_gate[0]
    w_up_mat = w_up[0]
    w_out_mat = w_out[0]
    micro_count, tok_rows, model_width = inputs_here.shape
    hidden_width = w_gate_mat.shape[1]
    token_scale = 1.0 / (micro_count * tok_rows)

    def backward(inputs_row, incoming):
        return section_back(inputs_row, incoming, gain_row, w_gate_mat, w_up_mat, w_out_mat)

    narrow_rows = jnp.zeros((micro_count, tok_rows, model_width), jnp.bfloat16)
    wide_rows = jnp.zeros((micro_count, tok_rows, hidden_width), jnp.bfloat16)
    store = (
        narrow_rows,
        wide_rows,
        wide_rows,
        wide_rows,
        narrow_rows,
        narrow_rows,
        jnp.zeros((model_width,), jnp.float32),
    )
    received = jnp.zeros((tok_rows, model_width), jnp.bfloat16)
    last_section = position == section_count - 1
    for clock_tick in range(micro_count + section_count - 1):
        micro_index = clock_tick - (section_count - 1 - position)
        active = jnp.logical_and(micro_index >= 0, micro_index < micro_count)
        safe_index = jnp.clip(micro_index, 0, micro_count - 1)

        def run_one(operand, safe_index=safe_index):
            arrived, previous = operand
            from_loss = lax.dynamic_index_in_dim(out_grad, safe_index, 0, keepdims=False)
            incoming = jnp.where(last_section, from_loss, arrived)
            inputs_row = lax.dynamic_index_in_dim(inputs_here, safe_index, 0, keepdims=False)
            passed, hidden_act, gate_grad, up_grad, normed, gain_term = backward(
                inputs_row, incoming
            )
            pieces = (passed, hidden_act, gate_grad, up_grad, normed, incoming)
            updated = tuple(
                (
                    lax.dynamic_update_index_in_dim(buffer, piece, safe_index, 0)
                    for buffer, piece in zip(previous[:6], pieces)
                )
            )
            return updated + (previous[6] + gain_term,)

        store = lax.cond(active, run_one, lambda operand: operand[1], (received, store))
        outgoing = lax.dynamic_index_in_dim(store[0], safe_index, 0, keepdims=False)
        received = from_behind(outgoing, "section", -1)
    hidden_flat = store[1].reshape(-1, hidden_width)
    gate_flat = store[2].reshape(-1, hidden_width)
    up_flat = store[3].reshape(-1, hidden_width)
    normed_flat = store[4].reshape(-1, model_width)
    incoming_flat = store[5].reshape(-1, model_width)
    contract = (((0,), (0,)), ((), ()))
    gate_part = lax.dot_general(
        normed_flat, gate_flat, contract, preferred_element_type=jnp.float32
    )
    up_part = lax.dot_general(normed_flat, up_flat, contract, preferred_element_type=jnp.float32)
    out_part = lax.dot_general(
        incoming_flat, hidden_flat, contract, preferred_element_type=jnp.float32
    )
    all_rows = scatter_axes(
        (jnp.concatenate([gate_part, up_part, out_part], axis=1) * token_scale).astype(
            jnp.bfloat16
        ),
        DP,
        (1, 2, 0),
        0,
    ).astype(jnp.float32)
    gate_rows = all_rows[:, :hidden_width]
    up_rows = all_rows[:, hidden_width : 2 * hidden_width]
    out_rows = all_rows[:, 2 * hidden_width :]
    gain_rows = sum_at_owner(store[6] * token_scale, DP, 0)
    return (gate_rows[None], up_rows[None], out_rows[None], gain_rows[None], store[0][None])


def solution(mesh):
    torus = Mesh(
        mesh.devices.reshape(mesh.shape["section"], 2, 4, 8), ("section", "dp_0", "dp_1", "dp_2")
    )
    return jax.shard_map(
        local,
        mesh=torus,
        in_specs=(
            P("section", None, DP, None),
            P("section", None),
            P("section", None, None),
            P("section", None, None),
            P("section", None, None),
            P(None, DP, None),
        ),
        out_specs=(
            P("section", DP, None),
            P("section", DP, None),
            P("section", DP, None),
            P("section", DP),
            P("section", None, DP, None),
        ),
        check_vma=False,
    )
```

profile of v0, /device:TPU:1, one launch (start us, length us, event | category | flops | bytes accessed | tf_op | source)
XLA Modules:
  0.0 292.5 jit_solution(8280886965020540636)
XLA Ops:
  7.2 5.4 %conditional.5 = (bf16[2,128,1024]{2,1,0:T(8,128)(2,1)}, bf16[2,128,1536]{2,1,0:T(8,128)(2,1)}, bf16[2,128,1536]{2,1,0:T(8,128)(2,1)}, bf16[2,128,1536]{2,1,0:T(...) conditional(s32[]{:T(128)} %convert_element_type.179, () %tuple.43, ...), branch_computations={%region_0.1_spmd, %region_1.5_spmd} | conditional | flops 2025717120 | bytes 76727576 | solution.py:134
  7.2 0.8 broadcast_in_dim.91.clone.1
  8.1 0.9 broadcast_in_dim.91.clone
  9.0 0.9 broadcast_in_dim.91
  9.8 0.9 broadcast_in_dim.92.clone.1
  10.7 1.0 broadcast_in_dim.92.clone
  11.7 0.9 broadcast_in_dim.92
  12.6 1.0 dynamic-slice_bitcast_fusion.3
  13.6 5.1 %collective-permute-start = (bf16[128,1024]{1,0:T(8,128)(2,1)S(1)}, bf16[128,1024]{1,0:T(8,128)(2,1)S(1)}, u32[]{:S(2)}, u32[]{:S(2)}) collective-permute-start(bf16[128,1024]{1,0:T(8,128)(2,1)S(1)} %dynamic-slice_bitcast_fusion.3), channel_id=1, source_target_pairs={{64,0},{128,64},{192,128},{65,1},{129,65},{193,129},{66,2},{130,66... | collective-permute-start | bytes 786440 | tf_op jit(solution)/shard_map/ppermute | solution.py:17
  18.7 5.1 %collective-permute-done = bf16[128,1024]{1,0:T(8,128)(2,1)S(1)} collective-permute-done((bf16[128,1024]{1,0:T(8,128)(2,1)S(1)}, bf16[128,1024]{1,0:T(8,128)(2,1)S(1)}, u32[]{:S(2)}, u32[]{:S(2)}) %collective-permute-start) | collective-permute-done | bytes 262176 | tf_op jit(solution)/shard_map/ppermute | solution.py:17
  23.9 1.0 dynamic-slice_bitcast_fusion.2
  24.8 1.9 collective-permute-start.1
  26.8 28.8 %collective-permute-done.1 = bf16[128,1024]{1,0:T(8,128)(2,1)S(1)} collective-permute-done((bf16[128,1024]{1,0:T(8,128)(2,1)S(1)}, bf16[128,1024]{1,0:T(8,128)(2,1)S(1)}, u32[]{:S(2)}, u32[]{:S(2)}) %collective-permute-start.1) | collective-permute-done | bytes 262176 | tf_op jit(solution)/shard_map/ppermute | solution.py:17
  55.6 12.3 %conditional.7 = ((bf16[2,128,1024]{2,1,0:T(8,128)(2,1)}, bf16[2,128,1536]{2,1,0:T(8,128)(2,1)}, bf16[2,128,1536]{2,1,0:T(8,128)(2,1)}, bf16[2,128,1536]{2,1,0:T...) conditional(s32[]{:T(128)} %convert_element_type.177, ...), branch_computations={%region_10.11_spmd, %region_11.15_spmd} | conditional | flops 2022375808 | bytes 69137184 | solution.py:134
  55.6 1.2 fusion.88
  56.8 2.6 fusion.107
  59.5 0.8 bitcast_dynamic-update-slice_fusion.7
  61.6 2.1 bitcast_dynamic-update-slice_fusion.6
  63.7 1.1 fusion.193
  64.8 0.8 copy-done.2
  65.5 1.3 fusion.97
  66.8 1.1 fusion.102
  67.9 1.0 dynamic-slice_bitcast_fusion.1
  68.9 1.9 collective-permute-start.2
  70.8 7.3 %collective-permute-done.2 = bf16[128,1024]{1,0:T(8,128)(2,1)S(1)} collective-permute-done((bf16[128,1024]{1,0:T(8,128)(2,1)S(1)}, bf16[128,1024]{1,0:T(8,128)(2,1)S(1)}, u32[]{:S(2)}, u32[]{:S(2)}) %collective-permute-start.2) | collective-permute-done | bytes 262176 | tf_op jit(solution)/shard_map/ppermute | solution.py:17
  78.1 12.4 %conditional.8 = ((bf16[2,128,1024]{2,1,0:T(8,128)(2,1)}, bf16[2,128,1536]{2,1,0:T(8,128)(2,1)}, bf16[2,128,1536]{2,1,0:T(8,128)(2,1)}, bf16[2,128,1536]{2,1,0:T...) conditional(s32[]{:T(128)} %convert_element_type.176, ...), branch_computations={%region_15.16_spmd, %region_16.20_spmd} | conditional | flops 2022375808 | bytes 69137184 | solution.py:134
  78.1 1.2 fusion.123
  79.3 2.6 fusion.142
  82.0 0.8 bitcast_dynamic-update-slice_fusion.10
  84.1 2.1 bitcast_dynamic-update-slice_fusion.9
  86.2 1.1 fusion.195
  87.3 0.8 copy-done.3
  88.1 1.3 fusion.132
  89.3 1.1 fusion.137
  90.4 1.0 dynamic-slice_bitcast_fusion
  91.4 1.9 collective-permute-start.3
  93.3 7.3 %collective-permute-done.3 = bf16[128,1024]{1,0:T(8,128)(2,1)S(1)} collective-permute-done((bf16[128,1024]{1,0:T(8,128)(2,1)S(1)}, bf16[128,1024]{1,0:T(8,128)(2,1)S(1)}, u32[]{:S(2)}, u32[]{:S(2)}) %collective-permute-start.3) | collective-permute-done | bytes 262176 | tf_op jit(solution)/shard_map/ppermute | solution.py:17
  100.6 2.3 fusion.196
  102.9 2.3 fusion.197
  105.2 2.3 fusion.198
  107.5 4.4 %fusion.182 = bf16[4,8,2,16,4608]{4,3,1,0,2:T(8,128)(2,1)} fusion(f32[2,4,8,16,1536]{4,3,2,1,0:T(8,128)S(1)} %bitcast.392, f32[2,4,8,16,1536]{4,3,2,1,0:T(8,128)S(1)} %bitcast.391, f32[2,4,8,16,1536]{4,3,2,1,0:T(8,128)S(1)} %bitcast.390), kind=kLoop, calls=%fused_computation.247 | loop fusion | flops 18874368 | bytes 28311552 | tf_op jit(solution)/shard_map/transpose | solution.py:23
  111.9 8.2 %copy.22 = bf16[4,8,2,16,4608]{4,3,2,1,0:T(8,128)(2,1)} copy(bf16[4,8,2,16,4608]{4,3,1,0,2:T(8,128)(2,1)} %fusion.182) | data formatting | bytes 18874368 | tf_op jit(solution)/shard_map/transpose | solution.py:23
  120.2 99.6 %reduce-scatter.4.cloned.1.call-done = bf16[16,16,4608]{2,1,0:T(8,128)(2,1)} async-done(((bf16[64,16,4608]{2,1,0:T(8,128)(2,1)}), bf16[16,16,4608]{2,1,0:T(8,128)(2,1)}) %reduce-scatter.4.cloned.1.call-update) | async-done | bytes 2359312 | tf_op jit(solution)/shard_map/reduce_scatter | solution.py:26
  219.8 40.9 %reduce-scatter.6.cloned.1.call-done = bf16[2,16,4608]{2,1,0:T(8,128)(2,1)} async-done(((bf16[16,16,4608]{2,1,0:T(8,128)(2,1)}), bf16[2,16,4608]{2,1,0:T(8,128)(2,1)}) %reduce-scatter.6.cloned.1.call-update) | async-done | bytes 294928 | tf_op jit(solution)/shard_map/reduce_scatter | solution.py:26
  260.8 19.0 %all_to_all.9 = f32[64,1,16]{2,1,0:T(1,128)S(1)} all-to-all(f32[64,1,16]{2,1,0:T(1,128)S(1)} %bitcast.415), channel_id=1, replica_groups=mesh['section'=4,'dp_0'=2,'dp_1'=4,'dp_2'=8] {'dp_0','dp_1','dp_2'}, dimensions={0} | all-to-all | bytes 8192 | tf_op jit(solution)/shard_map/all_to_all | solution.py:43
  280.5 3.9 %reduce-scatter.8.cloned.1.call-done = bf16[1,16,4608]{2,1,0:T(8,128)(2,1)} async-done(((bf16[2,16,4608]{2,1,0:T(8,128)(2,1)}), bf16[1,16,4608]{2,1,0:T(8,128)(2,1)}) %reduce-scatter.8.cloned.1.call-update) | async-done | bytes 147472 | tf_op jit(solution)/shard_map/reduce_scatter | solution.py:26
  284.3 0.9 bitcast_convert_fusion
  285.3 0.7 slice_bitcast_fusion
  (42 shorter events, 3.4 us)
Async XLA Ops:
  7.2 212.6 %reduce-scatter.4.cloned.1.call-start = ((), (), s32[]{:S(2)}) async-start(), calls=%async_computation.4 | async-start | bytes 11796480 | tf_op jit(solution)/shard_map/reduce_scatter | solution.py:26
  13.6 10.2 %collective-permute-start = (bf16[128,1024]{1,0:T(8,128)(2,1)S(1)}, bf16[128,1024]{1,0:T(8,128)(2,1)S(1)}, u32[]{:S(2)}, u32[]{:S(2)}) collective-permute-start(bf16[128,1024]{1,0:T(8,128)(2,1)S(1)} %dynamic-slice_bitcast_fusion.3), channel_id=1, source_target_pairs={{64,0},{128,64},{192,128},{65,1},{129,65},{193,129},{66,2},{130,66... | collective-permute-start | bytes 786440 | tf_op jit(solution)/shard_map/ppermute | solution.py:17
  24.8 30.7 %collective-permute-start.1 = (bf16[128,1024]{1,0:T(8,128)(2,1)S(1)}, bf16[128,1024]{1,0:T(8,128)(2,1)S(1)}, u32[]{:S(2)}, u32[]{:S(2)}) collective-permute-start(bf16[128,1024]{1,0:T(8,128)(2,1)S(1)} %dynamic-slice_bitcast_fusion.2), channel_id=1, source_target_pairs={{64,0},{128,64},{192,128},{65,1},{129,65},{193,129},{66,2},{130,66... | collective-permute-start | bytes 786440 | tf_op jit(solution)/shard_map/ppermute | solution.py:17
  55.6 4.7 %copy-start.18 = (bf16[1024,1536]{1,0:T(8,128)(2,1)S(1)}, bf16[1024,1536]{1,0:T(8,128)(2,1)}, u32[]{:S(2)}) copy-start(bf16[1024,1536]{1,0:T(8,128)(2,1)} %get-tuple-element.238) | copy-start | bytes 9437188 | tf_op jit(solution)/shard_map/cond
  55.6 3.9 %copy-start.23 = (bf16[2,128,1024]{2,1,0:T(8,128)(2,1)S(1)}, bf16[2,128,1024]{2,1,0:T(8,128)(2,1)}, u32[]{:S(2)}) copy-start(bf16[2,128,1024]{2,1,0:T(8,128)(2,1)} %get-tuple-element.234) | copy-start | bytes 1572868 | tf_op jit(solution)/shard_map/cond
  59.5 2.0 copy-start.7
  59.5 2.1 copy-start.13
  59.5 2.1 copy-start.27
  63.7 1.9 copy-start.2
  68.9 9.2 %collective-permute-start.2 = (bf16[128,1024]{1,0:T(8,128)(2,1)S(1)}, bf16[128,1024]{1,0:T(8,128)(2,1)S(1)}, u32[]{:S(2)}, u32[]{:S(2)}) collective-permute-start(bf16[128,1024]{1,0:T(8,128)(2,1)S(1)} %dynamic-slice_bitcast_fusion.1), channel_id=1, source_target_pairs={{64,0},{128,64},{192,128},{65,1},{129,65},{193,129},{66,2},{130,66... | collective-permute-start | bytes 786440 | tf_op jit(solution)/shard_map/ppermute | solution.py:17
  78.1 4.7 %copy-start.19 = (bf16[1024,1536]{1,0:T(8,128)(2,1)S(1)}, bf16[1024,1536]{1,0:T(8,128)(2,1)}, u32[]{:S(2)}) copy-start(bf16[1024,1536]{1,0:T(8,128)(2,1)} %get-tuple-element.254) | copy-start | bytes 9437188 | tf_op jit(solution)/shard_map/cond
  78.1 3.9 %copy-start.24 = (bf16[2,128,1024]{2,1,0:T(8,128)(2,1)S(1)}, bf16[2,128,1024]{2,1,0:T(8,128)(2,1)}, u32[]{:S(2)}) copy-start(bf16[2,128,1024]{2,1,0:T(8,128)(2,1)} %get-tuple-element.250) | copy-start | bytes 1572868 | tf_op jit(solution)/shard_map/cond
  82.0 2.0 copy-start.8
  82.0 2.1 copy-start.14
  82.0 2.1 copy-start.28
  86.2 1.9 copy-start.3
  91.4 9.2 %collective-permute-start.3 = (bf16[128,1024]{1,0:T(8,128)(2,1)S(1)}, bf16[128,1024]{1,0:T(8,128)(2,1)S(1)}, u32[]{:S(2)}, u32[]{:S(2)}) collective-permute-start(bf16[128,1024]{1,0:T(8,128)(2,1)S(1)} %dynamic-slice_bitcast_fusion), channel_id=1, source_target_pairs={{64,0},{128,64},{192,128},{65,1},{129,65},{193,129},{66,2},{130,66... | collective-permute-start | bytes 786440 | tf_op jit(solution)/shard_map/ppermute | solution.py:17
  120.1 140.6 %reduce-scatter.6.cloned.1.call-start = ((), (), s32[]{:S(2)}) async-start(), calls=%async_computation.5 | async-start | bytes 2654208 | tf_op jit(solution)/shard_map/reduce_scatter | solution.py:26
  219.8 64.5 %reduce-scatter.8.cloned.1.call-start = ((), (), s32[]{:S(2)}) async-start(), calls=%async_computation.6 | async-start | bytes 442368 | tf_op jit(solution)/shard_map/reduce_scatter | solution.py:26
Sparse Core Ops, SparseCore 0:
  120.3 99.4 reduce-scatter.3
  222.3 38.3 reduce-scatter.5
  263.2 21.1 reduce-scatter.7
where the time goes:
time: 293 us
  waiting for transfers between devices  193 us (66%)
  matrix products  22.3 us (8%)
  local copies, waits for them, and re-layouts  21.2 us (7%)
  blocking collectives  19 us (6%)
  between operations  13.9 us (5%)
  other arithmetic  12.1 us (4%)
  starting transfers between devices  11 us (4%)
    reduce_scatter x3, waiting for transfers between devices, reduced_to_own(): blocks = lax.psum_scatter(blocks, axes[k], scatter_dimension=0, tiled=True)  144 us
    ppermute x4, waiting for transfers between devices, from_behind(): lax.ppermute(value, axis, [(source, source + steps) for source in range(l...  48.4 us
    all_to_all x1, blocking collectives, sum_at_owner(): blocks = lax.all_to_all(split_up(x, dim, peers), axis, 0, 0, tiled=True)  19 us
    ppermute x4, starting transfers between devices, from_behind(): lax.ppermute(value, axis, [(source, source + steps) for source in range(l...  10.9 us
    transpose x1, local copies, waits for them, and re-layouts, reduced_to_own(): blocks = blocks.transpose(*order, *range(len(axes), blocks.ndim))  8.2 us
  transfers between devices with their start and end apart: 7, of which 7 were waited for; matrix products, arithmetic and copies ran while one was open for 0% of the time, Pallas kernels for 0%

commit v1 on v0

v1 whole, which is shorter than its diff:
```python
import jax
import jax.numpy as jnp
from jax import lax
from jax.experimental import pallas as pl
from jax.experimental.pallas import tpu as pltpu
from jax.sharding import Mesh
from jax.sharding import PartitionSpec as P

C_GELU = 0.7978845608028654
EPSILON = 1e-06
BLOCK = 256
BF16 = jnp.bfloat16
F32 = jnp.float32
DP = ("y", "x", "z")
VMEM_LIMIT = 48 * 1024 * 1024


def whole(shape):
    return pl.BlockSpec(shape, lambda *_: (0,) * len(shape))


def params():
    return pltpu.CompilerParams(
        dimension_semantics=("arbitrary",), vmem_limit_bytes=VMEM_LIMIT
    )


def inverse_rms_of(rows):
    return lax.rsqrt(jnp.mean(rows * rows, axis=-1, keepdims=True) + EPSILON)


def gelu_parts(pre_act):
    squared = pre_act * pre_act
    tangent = jnp.tanh(C_GELU * (pre_act + 0.044715 * squared * pre_act))
    half_open = 0.5 * (1.0 + tangent)
    slope = half_open + 0.5 * pre_act * (1.0 - tangent * tangent) * C_GELU * (
        1.0 + 3.0 * 0.044715 * squared
    )
    return (pre_act * half_open, slope)


def pre_kernel(x_ref, gain_ref, gate_ref, up_ref, normed_ref, hidden_ref, a_ref, b_ref):
    @pl.when(pl.program_id(0) == 0)
    def _():
        rows = x_ref[...].astype(F32)
        normed_ref[...] = (rows * inverse_rms_of(rows) * gain_ref[...]).astype(BF16)

    normed = normed_ref[...]
    gate_pre = jnp.dot(normed, gate_ref[...], preferred_element_type=F32)
    up_pre = jnp.dot(normed, up_ref[...], preferred_element_type=F32)
    value, slope = gelu_parts(gate_pre)
    hidden_ref[...] = (value * up_pre).astype(BF16)
    a_ref[...] = (up_pre * slope).astype(BF16)
    b_ref[...] = value.astype(BF16)


def pre(rows, gain_row, w_gate, w_up):
    count, width = rows.shape
    hid = w_gate.shape[1]
    column = lambda n: pl.BlockSpec((n, BLOCK), lambda j: (0, j))
    return pl.pallas_call(
        pre_kernel,
        grid=(hid // BLOCK,),
        in_specs=[whole((count, width)), whole((1, width)), column(width), column(width)],
        out_specs=[whole((count, width)), column(count), column(count), column(count)],
        out_shape=[jax.ShapeDtypeStruct((count, width), BF16)]
        + [jax.ShapeDtypeStruct((count, hid), BF16)] * 3,
        compiler_params=params(),
        cost_estimate=pl.CostEstimate(
            flops=4 * count * width * hid,
            bytes_accessed=4 * width * hid + 4 * count * width + 6 * count * hid,
            transcendentals=count * hid,
        ),
        name="pre",
    )(rows, gain_row, w_gate, w_up)


def tick_kernel(g_ref, x_ref, gain_ref, a_ref, b_ref, out_ref, gate_ref, up_ref, passed_ref, acc_ref):
    step = pl.program_id(0)
    act = jnp.dot(g_ref[...], out_ref[...], preferred_element_type=F32)
    gate_grad = (act * a_ref[...].astype(F32)).astype(BF16)
    up_grad = (act * b_ref[...].astype(F32)).astype(BF16)
    across = (((1,), (1,)), ((), ()))
    part = lax.dot_general(gate_grad, gate_ref[...], across, preferred_element_type=F32)
    part = part + lax.dot_general(up_grad, up_ref[...], across, preferred_element_type=F32)

    @pl.when(step == 0)
    def _():
        acc_ref[...] = part

    @pl.when(step > 0)
    def _():
        acc_ref[...] += part

    @pl.when(step == pl.num_programs(0) - 1)
    def _():
        rows = x_ref[...].astype(F32)
        inverse_rms = inverse_rms_of(rows)
        scaled = acc_ref[...] * gain_ref[...]
        mean = jnp.mean(scaled * rows, axis=-1, keepdims=True)
        grad = inverse_rms * scaled - rows * (inverse_rms * inverse_rms * inverse_rms * mean)
        passed_ref[...] = (g_ref[...].astype(F32) + grad).astype(BF16)


def tick(g, rows, micro, gain_row, a, b, w_out, w_gate, w_up):
    count, width = g.shape
    hid = w_gate.shape[1]
    weight = pl.BlockSpec((width, BLOCK), lambda j: (0, j))
    saved = pl.BlockSpec((count, BLOCK), lambda j: (micro, j))
    return pl.pallas_call(
        tick_kernel,
        grid=(hid // BLOCK,),
        in_specs=[
            whole((count, width)),
            pl.BlockSpec((count, width), lambda j: (micro, 0)),
            whole((1, width)),
            saved,
            saved,
            weight,
            weight,
            weight,
        ],
        out_specs=whole((count, width)),
        out_shape=jax.ShapeDtypeStruct((count, width), BF16),
        scratch_shapes=[pltpu.VMEM((count, width), F32)],
        compiler_params=params(),
        cost_estimate=pl.CostEstimate(
            flops=6 * count * width * hid, bytes_accessed=6 * width * hid, transcendentals=0
        ),
        name="tick",
    )(g, rows, gain_row, a, b, w_out, w_gate, w_up)


def weights_kernel(first, second):
    def kernel(
        place_ref, g0_ref, g1_ref, g2_ref, g3_ref, n_own_ref, n_pair_ref, h_own_ref, h_pair_ref,
        a_own_ref, a_pair_ref, b_own_ref, b_pair_ref, out_ref, send_ref, keep_ref,
        g_ref, tall_ref, nt_ref, gt_ref,
    ):
        quarter = g0_ref.shape[0]
        tokens, width = g_ref.shape
        half = width // 2
        slot = half // 4
        owner = slot // 8

        @pl.when(pl.program_id(0) == 0)
        def _():
            y, x, z = place_ref[0], place_ref[1], place_ref[2]
            for k, ref in enumerate((g0_ref, g1_ref, g2_ref, g3_ref)):
                g_ref[k * quarter : (k + 1) * quarter, :] = ref[...]

            def arrange(pick, target_ref):
                lower, upper = pick(slice(0, half)), pick(slice(half, width))
                mine = jnp.where(y == 0, lower.astype(F32), upper.astype(F32))
                tall_ref[...] = mine.T.astype(BF16)
                for k, mask in enumerate((first, first ^ second, 0, second)):
                    chunk = (x ^ mask) * slot
                    for d in range(8):
                        source = chunk + ((z + d) & 7) * owner
                        source = pl.multiple_of(source, owner)
                        start = k * slot + d * owner
                        target_ref[start : start + owner, :] = tall_ref[pl.ds(source, owner), :]

            arrange(lambda s: g_ref[:, s], gt_ref)
            arrange(lambda s: jnp.concatenate([n_own_ref[:, s], n_pair_ref[:, s]], axis=0), nt_ref)

        both = lambda one, other: jnp.concatenate([one[...], other[...]], axis=0)
        act = jnp.dot(g_ref[...], out_ref[...], preferred_element_type=F32)
        gate_grad = (act * both(a_own_ref, a_pair_ref).astype(F32)).astype(BF16)
        up_grad = (act * both(b_own_ref, b_pair_ref).astype(F32)).astype(BF16)
        hidden = both(h_own_ref, h_pair_ref)
        for t, (left_ref, right) in enumerate(
            ((nt_ref, gate_grad), (nt_ref, up_grad), (gt_ref, hidden))
        ):
            part = jnp.dot(left_ref[...], right, preferred_element_type=F32) * (1.0 / (2 * quarter))
            part = part.astype(BF16)
            for k in range(2):
                send_ref[t, k] = part[k * slot : (k + 1) * slot]
                keep_ref[t, k] = part[(k + 2) * slot : (k + 3) * slot]

    return kernel


def weight_grads(colour, masks, place, grads, normed, hidden, a, b, w_out):
    quarter, width = grads[0].shape
    hid = w_out.shape[1]
    steps = hid // BLOCK // 2
    tokens = 4 * quarter
    slot = width // 8
    full = lambda shape: pl.BlockSpec(shape, lambda j, _: (0,) * len(shape))
    saved = pl.BlockSpec((tokens // 2, BLOCK), lambda j, _: (0, colour * steps + j))
    piece = pl.BlockSpec((3, 2, slot, BLOCK), lambda j, _: (0, 0, 0, j))
    result = jax.ShapeDtypeStruct((3, 2, slot, hid // 2), BF16)
    return pl.pallas_call(
        weights_kernel(*masks),
        grid_spec=pltpu.PrefetchScalarGridSpec(
            num_scalar_prefetch=1,
            grid=(steps,),
            in_specs=[full((quarter, width))] * 4
            + [full((tokens // 2, width))] * 2
            + [saved] * 6
            + [pl.BlockSpec((width, BLOCK), lambda j, _: (0, colour * steps + j))],
            out_specs=[piece, piece],
            scratch_shapes=[
                pltpu.VMEM((tokens, width), BF16),
                pltpu.VMEM((width // 2, tokens), BF16),
                pltpu.VMEM((width // 2, tokens), BF16),
                pltpu.VMEM((width // 2, tokens), BF16),
            ],
        ),
        out_shape=[result, result],
        compiler_params=params(),
        cost_estimate=pl.CostEstimate(
            flops=5 * tokens * width * hid // 2,
            bytes_accessed=4 * width * hid + 6 * tokens * hid,
            transcendentals=0,
        ),
        name="weight_grads",
    )(place, *grads, *normed, *hidden, *a, *b, w_out)


def after(value, *others):
    return lax.optimization_barrier((value, *others))[0]


def local(section_inputs, gain, w_gate, w_up, w_out, out_grad):
    position = lax.axis_index("section")
    place = jnp.stack([lax.axis_index(a) for a in DP]).astype(jnp.int32)
    w_gate, w_up, w_out = w_gate[0], w_up[0], w_out[0]
    micro_count, tok_rows, width = section_inputs.shape[1:]
    hid = w_gate.shape[1]
    rows = section_inputs[0].reshape(micro_count * tok_rows, width)
    micros = range(micro_count)

    swap = [(0, 1), (1, 0)]
    rows_pair = lax.ppermute(rows, "y", swap)
    loss_pair = lax.ppermute(out_grad, ("section", "y"), [(6, 7), (7, 6)])
    normed, hidden, a, b = pre(rows, gain, w_gate, w_up)

    def run(section, micro, g, held):
        return lax.cond(
            position == section,
            lambda: tick(g, rows, micro, gain, a, b, w_out, w_gate, w_up),
            lambda: held,
        )

    def hop(value, section, crossed):
        pairs = [(2 * (section + 1) + y, 2 * section + (y ^ crossed)) for y in range(2)]
        return lax.ppermute(value, ("section", "y"), pairs)

    passed = [run(3, m, out_grad[m], out_grad[m]) for m in micros]
    rows_pair = after(rows_pair, passed[1])
    normed_pair, hidden_pair, a_pair, b_pair = pre(rows_pair, gain, w_gate, w_up)
    own = [out_grad[m] for m in micros]
    pair = [loss_pair[m] for m in micros]
    for section in (2, 1, 0):
        here = position == section
        arrived = [hop(passed[m], section, 0) for m in micros]
        if section == 1:
            crossed = [
                lax.ppermute(arrived[m], ("section", "y"), [(2, 3), (3, 2)]) for m in micros
            ]
        else:
            crossed = [hop(passed[m], section, 1) for m in micros]
        own = [jnp.where(here, arrived[m], own[m]) for m in micros]
        pair = [jnp.where(here, crossed[m], pair[m]) for m in micros]
        if section:
            passed = [run(section, m, arrived[m], passed[m]) for m in micros]

    masks = ((1, 3), (3, 1))
    parts = [
        weight_grads(
            colour, masks[colour], place, (*own, *pair), (normed, normed_pair),
            (hidden, hidden_pair), (a, a_pair), (b, b_pair), w_out,
        )
        for colour in range(2)
    ]
    late = [after(arrived[0], parts[0][0]), after(arrived[1], parts[1][0])]
    passed = [run(0, m, late[m], passed[m]) for m in micros]

    summed = []
    for colour in range(2):
        first, second = masks[colour]
        to = lambda mask: [(i, i ^ mask) for i in range(4)]
        send, keep = parts[colour]
        keep = keep + lax.ppermute(send, "x", to(first))
        got = lax.ppermute(keep[:, 1], "x", to(second))
        summed.append(keep[:, 0] + got)
    summed = jnp.stack(summed)
    owned = summed.shape[2] // 8
    pieces = [summed[:, :, d * owned : (d + 1) * owned] for d in range(8)]
    total = pieces[0].astype(F32)
    for d in range(1, 8):
        got = lax.ppermute(pieces[d], "z", [(i, (i + d) % 8) for i in range(8)])
        total = total + got.astype(F32)
    grad_gate, grad_up, grad_out = [
        jnp.concatenate([total[0, t], total[1, t]], axis=-1) for t in range(3)
    ]
    start = lax.axis_index(DP) * owned
    mine = lambda w: lax.dynamic_slice_in_dim(w, start, owned, 0).astype(F32)
    dots = jnp.sum(mine(w_gate) * grad_gate + mine(w_up) * grad_up, axis=-1)
    grad_gain = dots / lax.dynamic_slice_in_dim(gain[0], start, owned, 0)
    return (
        grad_gate[None],
        grad_up[None],
        grad_out[None],
        grad_gain[None],
        jnp.stack(passed)[None],
    )


def solution(mesh):
    torus = Mesh(mesh.devices.reshape(4, 2, 4, 8), ("section", *DP))
    return jax.shard_map(
        local,
        mesh=torus,
        in_specs=(
            P("section", None, DP, None),
            P("section", None),
            P("section", None, None),
            P("section", None, None),
            P("section", None, None),
            P(None, DP, None),
        ),
        out_specs=(
            P("section", DP, None),
            P("section", DP, None),
            P("section", DP, None),
            P("section", DP),
            P("section", None, DP, None),
        ),
        check_vma=False,
    )
```

time: 293 us -> 180 us (0.61)
  waiting for transfers between devices: 193 us -> 77.2 us
  Pallas kernels: 0 us -> 42.1 us
  starting transfers between devices: 11 us -> 41.2 us
  matrix products: 22.3 us -> 0 us
  blocking collectives: 19 us -> 0 us
  local copies, waits for them, and re-layouts: 21.2 us -> 7.03 us
  between operations: 13.9 us -> 1.03 us
    reduce_scatter x3 -> x0, waiting for transfers between devices: 144 us -> none  [reduced_to_own(): blocks = lax.psum_scatter(blocks, axes[k], scatter_dimension=0, tiled=True)]
    pallas_call x0 -> x6, Pallas kernels: none -> 42.1 us  [the longest x2 17.2 us: tick(): pl.pallas_call(tick_kernel, grid=(hid // BLOCK,), in_specs=[whole((count,...]
    ppermute x4 -> x25, starting transfers between devices: 10.9 us -> 41.2 us  [the longest x7 15.7 us: local(): got = lax.ppermute(pieces[d], 'z', [(i, (i + d) % 8) for i in range(8)])]
    ppermute x4 -> x25, waiting for transfers between devices: 48.4 us -> 77.2 us  [the longest x2 27.2 us: local(): keep = keep + lax.ppermute(send, 'x', to(first))]
    dot_general x13 -> x0, matrix products: 22.3 us -> none  [the longest x2 5.28 us: section_back(): up_pre = jnp.dot(normed, w_up_mat, preferred_element_type=jnp.float32)]
    all_to_all x1 -> x0, blocking collectives: 19 us -> none  [sum_at_owner(): blocks = lax.all_to_all(split_up(x, dim, peers), axis, 0, 0, tiled=True)]
    transpose x1 -> x0, local copies, waits for them, and re-layouts: 8.2 us -> none  [reduced_to_own(): blocks = blocks.transpose(*order, *range(len(axes), blocks.ndim))]
    broadcast_in_dim x8 -> x0, local copies, waits for them, and re-layouts: 6.11 us -> none  [the longest x3 2.83 us: local(): wide_rows = jnp.zeros((micro_count, tok_rows, hidden_width), jnp.bfloat16)]
  transfers between devices with their start and end apart: 7 -> 25, of which waited for: 7 -> 12; matrix products, arithmetic and copies ran while one was open for 0% -> 5% of each run, Pallas kernels for 0% -> 17%
where the time goes in v1:
time: 180 us; the launch traced here: 179 us
  waiting for transfers between devices  77.2 us (43%)
  Pallas kernels  42.1 us (23%)
  starting transfers between devices  41.2 us (23%)
  other arithmetic  10.2 us (6%)
  local copies, waits for them, and re-layouts  7.03 us (4%)
    ppermute x2, waiting for transfers between devices, local(): keep = keep + lax.ppermute(send, 'x', to(first))  27.2 us
    ppermute x10, waiting for transfers between devices, hop(): return lax.ppermute(value, ('section', 'y'), pairs)  18.7 us
    pallas_call x2, Pallas kernels, tick(): pl.pallas_call(tick_kernel, grid=(hid // BLOCK,), in_specs=[whole((count,...  17.2 us
    ppermute x7, waiting for transfers between devices, local(): got = lax.ppermute(pieces[d], 'z', [(i, (i + d) % 8) for i in range(8)])  16.6 us
    ppermute x7, starting transfers between devices, local(): got = lax.ppermute(pieces[d], 'z', [(i, (i + d) % 8) for i in range(8)])  15.7 us
    ppermute x10, starting transfers between devices, hop(): return lax.ppermute(value, ('section', 'y'), pairs)  13.3 us
    pallas_call x2, Pallas kernels, pre(): pl.pallas_call(pre_kernel, grid=(hid // BLOCK,), in_specs=[whole((count,...  13 us
    pallas_call x2, Pallas kernels, weight_grads(): pl.pallas_call(weights_kernel(*masks), grid_spec=pltpu.PrefetchScalarGrid...  11.8 us
  transfers between devices with their start and end apart: 25, of which 12 were waited for; matrix products, arithmetic and copies ran while one was open for 5% of the time, Pallas kernels for 17%

profile of v1, /device:TPU:1, one launch (start us, length us, event | category | flops | bytes accessed | tf_op | source)
XLA Modules:
  0.0 178.9 jit_solution(2924721826628245662)
XLA Ops:
  0.6 1.9 %slice_bitcast_fusion.6 = (bf16[128,1024]{1,0:T(8,128)(2,1)}, bf16[128,1024]{1,0:T(8,128)(2,1)}) fusion(bf16[2,128,1024]{2,1,0:T(8,128)(2,1)} %param.27), kind=kLoop, calls=%fused_computation.34 | loop fusion | bytes 1048576 | tf_op jit(solution)/shard_map/squeeze | solution.py:251
  2.6 6.5 %pre.2 = (bf16[256,1024]{1,0:T(8,128)(2,1)S(1)}, bf16[256,1536]{1,0:T(8,128)(2,1)S(1)}, bf16[256,1536]{1,0:T(8,128)(2,1)S(1)}, bf16[256,1536]{1,0:T(8,128)(2,1)S(1)}) custom-call(bf16[256,1024]{1,0:T(8,128)(2,1)S(1)} %bitcast.120, f32[1,1024]{1,0:T(1,128)} %gain_ref.3, bf16[1024,1536]{1,0:T(8,128)(2,1)} %bitcast.83, bf16[1024,1536]{1,0:T(8,128)(2,1)} %bitcast.93), custom_call_target="tpu_custom_call" | custom-call | flops 1610612736 | bytes 9699328 | tf_op jit(solution)/shard_map/pre/pallas_call | solution.py:61
  9.1 1.4 collective-permute-start
  10.5 1.4 collective-permute-start.3
  11.9 2.1 %collective-permute-start.13 = (bf16[256,1024]{1,0:T(8,128)(2,1)}, bf16[256,1024]{1,0:T(8,128)(2,1)S(1)}, u32[]{:S(2)}, u32[]{:S(2)}) collective-permute-start(bf16[256,1024]{1,0:T(8,128)(2,1)} %bitcast.113), channel_id=1, source_target_pairs={{0,32},{32,0},{1,33},{33,1},{2,34},{34,2},{3,35},{35,3},{4,36},{36... | collective-permute-start | bytes 1572872 | tf_op jit(solution)/shard_map/ppermute | solution.py:236
  14.0 1.7 conditional.9
  14.0 1.7 copy.24
  16.9 1.7 conditional.12
  17.0 1.7 copy.18
  19.9 1.4 collective-permute-start.12
  21.3 1.4 collective-permute-start.8
  22.7 18.7 %collective-permute-done.1 = bf16[128,1024]{1,0:T(8,128)(2,1)} collective-permute-done((bf16[128,1024]{1,0:T(8,128)(2,1)}, bf16[128,1024]{1,0:T(8,128)(2,1)}, u32[]{:S(2)}, u32[]{:S(2)}) %collective-permute-start.1) | collective-permute-done | bytes 262176 | tf_op jit(solution)/shard_map/ppermute | solution.py:249
  41.4 1.5 collective-permute-start.9
  42.9 8.6 %conditional.10 = (bf16[128,1024]{1,0:T(8,128)(2,1)}) conditional(s32[]{:T(128)} %convert_element_type.52, bf16[128,1024]{1,0:T(8,128)(2,1)} %get-tuple-element.302, (bf16[128,1024]{1,0:T(8,128)(2,1)}, bf16[256,1024]{1,0:T(8,128)(2,1)}, f32[1,1024]{1,0:T(1,128)S(1)}, bf16[256,1536]{1,0:T(8,128)(2,1)S(1)}, bf16[256,1536]{1,0:T(8,128)(2,1)S(1)}, ...), branch_computations={%region_4.5_spmd, %region_5.6_spmd} | conditional | flops 1207959552 | bytes 9437192 | solution.py:241
  42.9 8.6 %tick.10 = bf16[128,1024]{1,0:T(8,128)(2,1)} custom-call(bf16[128,1024]{1,0:T(8,128)(2,1)} %get-tuple-element.188.g_ref, bf16[256,1024]{1,0:T(8,128)(2,1)} %get-tuple-element.189.x_ref, f32[1,1024]{1,0:T(1,128)S(1)} %get-tuple-element.190.gain_ref, bf16[256,1536]{1,0:T(8,128)(2,1)S(1)} %get-tuple-element.191.a_ref, ...), custom_call_target="tpu_custom_call" | custom-call | flops 1207959552 | bytes 9437184 | tf_op jit(solution)/shard_map/cond/branch_1_fun/tick/pallas_call | solution.py:110
  51.5 8.6 %conditional.13 = (bf16[128,1024]{1,0:T(8,128)(2,1)}) conditional(s32[]{:T(128)} %convert_element_type.52, bf16[128,1024]{1,0:T(8,128)(2,1)} %get-tuple-element.305, (bf16[128,1024]{1,0:T(8,128)(2,1)}, bf16[256,1024]{1,0:T(8,128)(2,1)}, f32[1,1024]{1,0:T(1,128)S(1)}, bf16[256,1536]{1,0:T(8,128)(2,1)S(1)}, bf16[256,1536]{1,0:T(8,128)(2,1)S(1)}, ...), branch_computations={%region_10.11_spmd, %region_11.12_spmd} | conditional | flops 1207959552 | bytes 9437192 | solution.py:241
  51.5 8.6 %tick.13 = bf16[128,1024]{1,0:T(8,128)(2,1)} custom-call(bf16[128,1024]{1,0:T(8,128)(2,1)} %get-tuple-element.212.g_ref, bf16[256,1024]{1,0:T(8,128)(2,1)} %get-tuple-element.213.x_ref, f32[1,1024]{1,0:T(1,128)S(1)} %get-tuple-element.214.gain_ref, bf16[256,1536]{1,0:T(8,128)(2,1)S(1)} %get-tuple-element.215.a_ref, ...), custom_call_target="tpu_custom_call" | custom-call | flops 1207959552 | bytes 9437184 | tf_op jit(solution)/shard_map/cond/branch_1_fun/tick/pallas_call | solution.py:110
  60.1 1.3 collective-permute-start.2
  61.4 1.3 collective-permute-start.5
  62.8 6.5 %pre.3 = (bf16[256,1024]{1,0:T(8,128)(2,1)S(1)}, bf16[256,1536]{1,0:T(8,128)(2,1)S(1)}, bf16[256,1536]{1,0:T(8,128)(2,1)S(1)}, bf16[256,1536]{1,0:T(8,128)(2,1)S(1)}) custom-call(bf16[256,1024]{1,0:T(8,128)(2,1)S(1)} %collective-permute-done.13.x_ref, f32[1,1024]{1,0:T(1,128)S(1)} %copy-done.16, bf16[1024,1536]{1,0:T(8,128)(2,1)} %bitcast.90, ...), custom_call_target="tpu_custom_call" | custom-call | flops 1610612736 | bytes 9699328 | tf_op jit(solution)/shard_map/pre/pallas_call | solution.py:61
  69.4 1.3 collective-permute-start.6
  70.7 1.3 collective-permute-start.10
  72.0 2.8 %collective-permute-start.7 = (bf16[128,1024]{1,0:T(8,128)(2,1)}, bf16[128,1024]{1,0:T(8,128)(2,1)S(1)}, u32[]{:S(2)}, u32[]{:S(2)}) collective-permute-start(bf16[128,1024]{1,0:T(8,128)(2,1)} %collective-permute-done.1), channel_id=1, source_target_pairs={{64,96},{96,64},{65,97},{97,65},{66,98},{98,66},{67,99},{99,67},{6... | collective-permute-start | bytes 786440 | tf_op jit(solution)/shard_map/ppermute | solution.py:261
  74.9 2.4 %collective-permute-start.11 = (bf16[128,1024]{1,0:T(8,128)(2,1)}, bf16[128,1024]{1,0:T(8,128)(2,1)S(1)}, u32[]{:S(2)}, u32[]{:S(2)}) collective-permute-start(bf16[128,1024]{1,0:T(8,128)(2,1)} %collective-permute-done.4), channel_id=1, source_target_pairs={{64,96},{96,64},{65,97},{97,65},{66,98},{98,66},{67,99},{99,67},{6... | collective-permute-start | bytes 786440 | tf_op jit(solution)/shard_map/ppermute | solution.py:261
  77.4 1.3 select_select_fusion
  78.8 2.2 %collective-permute-done.7 = bf16[128,1024]{1,0:T(8,128)(2,1)S(1)} collective-permute-done((bf16[128,1024]{1,0:T(8,128)(2,1)}, bf16[128,1024]{1,0:T(8,128)(2,1)S(1)}, u32[]{:S(2)}, u32[]{:S(2)}) %collective-permute-start.7) | collective-permute-done | bytes 262176 | tf_op jit(solution)/shard_map/ppermute | solution.py:261
  81.0 2.8 %collective-permute-done.11 = bf16[128,1024]{1,0:T(8,128)(2,1)S(1)} collective-permute-done((bf16[128,1024]{1,0:T(8,128)(2,1)}, bf16[128,1024]{1,0:T(8,128)(2,1)S(1)}, u32[]{:S(2)}, u32[]{:S(2)}) %collective-permute-start.11) | collective-permute-done | bytes 262176 | tf_op jit(solution)/shard_map/ppermute | solution.py:261
  84.9 5.9 %weight_grads.3 = (bf16[3,2,128,768]{3,2,1,0:T(8,128)(2,1)}, bf16[3,2,128,768]{3,2,1,0:T(8,128)(2,1)}) custom-call(s32[3]{0:T(128)S(1)} %pad_add_fusion.place_ref, bf16[128,1024]{1,0:T(8,128)(2,1)S(1)} %get-tuple-element.285.g0_ref, bf16[128,1024]{1,0:T(8,128)(2,1)S(1)} %get-tuple-element.284.g1_ref, bf16[128,1024]{1,0:T(8,128)(2,1)S(1)} %get-tuple-element.283.g2_ref, ...), custom_call_target="tpu_custom_call" | custom-call | flops 2013265920 | bytes 11010048 | tf_op jit(solution)/shard_map/weight_grads/pallas_call | solution.py:194
  90.9 2.5 %collective-permute-start.16 = (bf16[3,2,128,768]{3,2,1,0:T(8,128)(2,1)}, bf16[3,2,128,768]{3,2,1,0:T(8,128)(2,1)S(1)}, u32[]{:S(2)}, u32[]{:S(2)}) collective-permute-start(bf16[3,2,128,768]{3,2,1,0:T(8,128)(2,1)} %get-tuple-element.268), channel_id=1, source_target_pairs={{0,24},{8,16},{16,8},{24,0},{1,25},{9,17},{17,9},{25,1},{2,26},{10... | collective-permute-start | bytes 3538952 | tf_op jit(solution)/shard_map/ppermute | solution.py:286
  93.4 5.9 %weight_grads.2 = (bf16[3,2,128,768]{3,2,1,0:T(8,128)(2,1)}, bf16[3,2,128,768]{3,2,1,0:T(8,128)(2,1)}) custom-call(s32[3]{0:T(128)S(1)} %pad_add_fusion.place_ref, bf16[128,1024]{1,0:T(8,128)(2,1)S(1)} %get-tuple-element.285.g0_ref, bf16[128,1024]{1,0:T(8,128)(2,1)S(1)} %get-tuple-element.284.g1_ref, bf16[128,1024]{1,0:T(8,128)(2,1)S(1)} %get-tuple-element.283.g2_ref, ...), custom_call_target="tpu_custom_call" | custom-call | flops 2013265920 | bytes 11010048 | tf_op jit(solution)/shard_map/weight_grads/pallas_call | solution.py:194
  99.3 1.4 copy.11
  101.0 14.5 %collective-permute-done.16 = bf16[3,2,128,768]{3,2,1,0:T(8,128)(2,1)S(1)} collective-permute-done((bf16[3,2,128,768]{3,2,1,0:T(8,128)(2,1)}, bf16[3,2,128,768]{3,2,1,0:T(8,128)(2,1)S(1)}, u32[]{:S(2)}, u32[]{:S(2)}) %collective-permute-start.16) | collective-permute-done | bytes 1179680 | tf_op jit(solution)/shard_map/ppermute | solution.py:286
  116.3 12.7 %collective-permute-done.14 = bf16[3,2,128,768]{3,2,0,1:T(8,128)(2,1)S(1)} collective-permute-done((bf16[3,2,128,768]{3,2,0,1:T(8,128)(2,1)S(1)}, bf16[3,2,128,768]{3,2,0,1:T(8,128)(2,1)S(1)}, u32[]{:S(2)}, u32[]{:S(2)}) %collective-permute-start.14) | collective-permute-done | bytes 1179680 | tf_op jit(solution)/shard_map/ppermute | solution.py:286
  129.4 7.7 %collective-permute-done.17 = bf16[3,128,768]{2,1,0:T(8,128)(2,1)S(1)} collective-permute-done((bf16[3,128,768]{2,1,0:T(8,128)(2,1)S(1)}, bf16[3,128,768]{2,1,0:T(8,128)(2,1)S(1)}, u32[]{:S(2)}, u32[]{:S(2)}) %collective-permute-start.17) | collective-permute-done | bytes 589856 | tf_op jit(solution)/shard_map/ppermute | solution.py:287
  137.2 2.0 %collective-permute-done.15 = bf16[3,128,768]{2,1,0:T(8,128)(2,1)S(1)} collective-permute-done((bf16[3,128,768]{2,1,0:T(8,128)(2,1)S(1)}, bf16[3,128,768]{2,1,0:T(8,128)(2,1)S(1)}, u32[]{:S(2)}, u32[]{:S(2)}) %collective-permute-start.15) | collective-permute-done | bytes 589856 | tf_op jit(solution)/shard_map/ppermute | solution.py:287
  140.3 1.6 collective-permute-start.18
  141.9 3.0 %collective-permute-start.19 = (bf16[2,3,16,768]{3,2,1,0:T(8,128)(2,1)S(1)}, bf16[2,3,16,768]{3,2,1,0:T(8,128)(2,1)}, u32[]{:S(2)}, u32[]{:S(2)}) collective-permute-start(bf16[2,3,16,768]{3,2,1,0:T(8,128)(2,1)S(1)} %get-tuple-element.276), channel_id=1, source_target_pairs={{0,2},{1,3},{2,4},{3,5},{4,6},{5,7},{6,0},{7,1},{8,10},{9,11},{10,... | collective-permute-start | bytes 442376 | tf_op jit(solution)/shard_map/ppermute | solution.py:294
  144.9 3.8 %collective-permute-start.20 = (bf16[2,3,16,768]{3,2,1,0:T(8,128)(2,1)}, bf16[2,3,16,768]{3,2,1,0:T(8,128)(2,1)}, u32[]{:S(2)}, u32[]{:S(2)}) collective-permute-start(bf16[2,3,16,768]{3,2,1,0:T(8,128)(2,1)} %get-tuple-element.277), channel_id=1, source_target_pairs={{0,3},{1,4},{2,5},{3,6},{4,7},{5,0},{6,1},{7,2},{8,11},{9,12},{10,... | collective-permute-start | bytes 442376 | tf_op jit(solution)/shard_map/ppermute | solution.py:294
  149.2 4.5 %collective-permute-start.22 = (bf16[2,3,16,768]{3,2,1,0:T(8,128)(2,1)}, bf16[2,3,16,768]{3,2,1,0:T(8,128)(2,1)}, u32[]{:S(2)}, u32[]{:S(2)}) collective-permute-start(bf16[2,3,16,768]{3,2,1,0:T(8,128)(2,1)} %get-tuple-element.279), channel_id=1, source_target_pairs={{0,5},{1,6},{2,7},{3,0},{4,1},{5,2},{6,3},{7,4},{8,13},{9,14},{10,... | collective-permute-start | bytes 442376 | tf_op jit(solution)/shard_map/ppermute | solution.py:294
  153.6 2.4 %collective-permute-start.23 = (bf16[2,3,16,768]{3,2,1,0:T(8,128)(2,1)}, bf16[2,3,16,768]{3,2,1,0:T(8,128)(2,1)}, u32[]{:S(2)}, u32[]{:S(2)}) collective-permute-start(bf16[2,3,16,768]{3,2,1,0:T(8,128)(2,1)} %get-tuple-element.281), channel_id=1, source_target_pairs={{0,6},{1,7},{2,0},{3,1},{4,2},{5,3},{6,4},{7,5},{8,14},{9,15},{10,... | collective-permute-start | bytes 442376 | tf_op jit(solution)/shard_map/ppermute | solution.py:294
  156.0 6.7 %collective-permute-done.19 = bf16[2,3,16,768]{3,2,1,0:T(8,128)(2,1)} collective-permute-done((bf16[2,3,16,768]{3,2,1,0:T(8,128)(2,1)S(1)}, bf16[2,3,16,768]{3,2,1,0:T(8,128)(2,1)}, u32[]{:S(2)}, u32[]{:S(2)}) %collective-permute-start.19) | collective-permute-done | bytes 147488 | tf_op jit(solution)/shard_map/ppermute | solution.py:294
  162.7 1.9 %maximum_bitcast_fusion = bf16[1,2,128,1024]{3,2,1,0:T(8,128)(2,1)} fusion(bf16[1,128,1024]{2,1,0:T(8,128)(2,1)} %bitcast.124, bf16[1,128,1024]{2,1,0:T(8,128)(2,1)S(1)} %bitcast.123), kind=kLoop, calls=%fused_computation.23 | loop fusion | flops 262144 | bytes 1048576 | tf_op jit(solution)/shard_map/broadcast_in_dim | solution.py:308
  164.6 2.5 %collective-permute-done.20 = bf16[2,3,16,768]{3,2,1,0:T(8,128)(2,1)} collective-permute-done((bf16[2,3,16,768]{3,2,1,0:T(8,128)(2,1)}, bf16[2,3,16,768]{3,2,1,0:T(8,128)(2,1)}, u32[]{:S(2)}, u32[]{:S(2)}) %collective-permute-start.20) | collective-permute-done | bytes 147488 | tf_op jit(solution)/shard_map/ppermute | solution.py:294
  167.1 3.1 %collective-permute-done.22 = bf16[2,3,16,768]{3,2,1,0:T(8,128)(2,1)} collective-permute-done((bf16[2,3,16,768]{3,2,1,0:T(8,128)(2,1)}, bf16[2,3,16,768]{3,2,1,0:T(8,128)(2,1)}, u32[]{:S(2)}, u32[]{:S(2)}) %collective-permute-start.22) | collective-permute-done | bytes 147488 | tf_op jit(solution)/shard_map/ppermute | solution.py:294
  170.2 1.9 %collective-permute-done.23 = bf16[2,3,16,768]{3,2,1,0:T(8,128)(2,1)} collective-permute-done((bf16[2,3,16,768]{3,2,1,0:T(8,128)(2,1)}, bf16[2,3,16,768]{3,2,1,0:T(8,128)(2,1)}, u32[]{:S(2)}, u32[]{:S(2)}) %collective-permute-start.23) | collective-permute-done | bytes 147488 | tf_op jit(solution)/shard_map/ppermute | solution.py:294
  172.1 2.5 %collective-permute-done.24 = bf16[2,3,16,768]{3,2,1,0:T(8,128)(2,1)} collective-permute-done((bf16[2,3,16,768]{3,2,1,0:T(8,128)(2,1)}, bf16[2,3,16,768]{3,2,1,0:T(8,128)(2,1)}, u32[]{:S(2)}, u32[]{:S(2)}) %collective-permute-start.24) | collective-permute-done | bytes 147488 | tf_op jit(solution)/shard_map/ppermute | solution.py:294
  174.5 1.5 convert_add_fusion
  176.0 1.6 fusion.18
  (70 shorter events, 8.3 us)
Async XLA Ops:
  0.6 1.9 %copy-start.4 = (bf16[1,2,128,1024]{3,2,1,0:T(8,128)(2,1)S(1)}, bf16[1,2,128,1024]{3,2,1,0:T(8,128)(2,1)}, u32[]{:S(2)}) copy-start(bf16[1,2,128,1024]{3,2,1,0:T(8,128)(2,1)} %param.22) | copy-start | bytes 1572868
  2.6 6.6 %copy-start.16 = (f32[1,1024]{1,0:T(1,128)S(1)}, f32[1,1024]{1,0:T(1,128)}, u32[]{:S(2)}) copy-start(f32[1,1024]{1,0:T(1,128)} %gain_ref.3) | copy-start | bytes 12292
  9.1 84.3 %copy-start.2 = (bf16[256,1536]{1,0:T(8,128)(2,1)}, bf16[256,1536]{1,0:T(8,128)(2,1)S(1)}, u32[]{:S(2)}) copy-start(bf16[256,1536]{1,0:T(8,128)(2,1)S(1)} %get-tuple-element.256.a_own_ref) | copy-start | bytes 2359300
  9.1 84.3 %copy-start.3 = (bf16[256,1536]{1,0:T(8,128)(2,1)}, bf16[256,1536]{1,0:T(8,128)(2,1)S(1)}, u32[]{:S(2)}) copy-start(bf16[256,1536]{1,0:T(8,128)(2,1)S(1)} %get-tuple-element.257.b_own_ref) | copy-start | bytes 2359300
  9.1 4.8 %collective-permute-start = (bf16[128,1024]{1,0:T(8,128)(2,1)}, bf16[128,1024]{1,0:T(8,128)(2,1)}, u32[]{:S(2)}, u32[]{:S(2)}) collective-permute-start(bf16[128,1024]{1,0:T(8,128)(2,1)} %get-tuple-element.301), channel_id=1, source_target_pairs={{192,128},{224,160},{193,129},{225,161},{194,130},{226,162},{195,1... | collective-permute-start | bytes 786440 | tf_op jit(solution)/shard_map/ppermute | solution.py:249
  10.5 6.4 %collective-permute-start.3 = (bf16[128,1024]{1,0:T(8,128)(2,1)}, bf16[128,1024]{1,0:T(8,128)(2,1)}, u32[]{:S(2)}, u32[]{:S(2)}) collective-permute-start(bf16[128,1024]{1,0:T(8,128)(2,1)} %get-tuple-element.304), channel_id=1, source_target_pairs={{192,128},{224,160},{193,129},{225,161},{194,130},{226,162},{195,1... | collective-permute-start | bytes 786440 | tf_op jit(solution)/shard_map/ppermute | solution.py:249
  11.9 49.5 %collective-permute-start.13 = (bf16[256,1024]{1,0:T(8,128)(2,1)}, bf16[256,1024]{1,0:T(8,128)(2,1)S(1)}, u32[]{:S(2)}, u32[]{:S(2)}) collective-permute-start(bf16[256,1024]{1,0:T(8,128)(2,1)} %bitcast.113), channel_id=1, source_target_pairs={{0,32},{32,0},{1,33},{33,1},{2,34},{34,2},{3,35},{35,3},{4,36},{36... | collective-permute-start | bytes 1572872 | tf_op jit(solution)/shard_map/ppermute | solution.py:236
  15.6 25.7 %collective-permute-start.1 = (bf16[128,1024]{1,0:T(8,128)(2,1)}, bf16[128,1024]{1,0:T(8,128)(2,1)}, u32[]{:S(2)}, u32[]{:S(2)}) collective-permute-start(bf16[128,1024]{1,0:T(8,128)(2,1)} %get-tuple-element.302), channel_id=1, source_target_pairs={{128,64},{160,96},{129,65},{161,97},{130,66},{162,98},{131,67},{16... | collective-permute-start | bytes 786440 | tf_op jit(solution)/shard_map/ppermute | solution.py:249
  18.6 32.9 %collective-permute-start.4 = (bf16[128,1024]{1,0:T(8,128)(2,1)}, bf16[128,1024]{1,0:T(8,128)(2,1)}, u32[]{:S(2)}, u32[]{:S(2)}) collective-permute-start(bf16[128,1024]{1,0:T(8,128)(2,1)} %get-tuple-element.305), channel_id=1, source_target_pairs={{128,64},{160,96},{129,65},{161,97},{130,66},{162,98},{131,67},{16... | collective-permute-start | bytes 786440 | tf_op jit(solution)/shard_map/ppermute | solution.py:249
  19.9 49.4 %collective-permute-start.12 = (bf16[128,1024]{1,0:T(8,128)(2,1)}, bf16[128,1024]{1,0:T(8,128)(2,1)}, u32[]{:S(2)}, u32[]{:S(2)}) collective-permute-start(bf16[128,1024]{1,0:T(8,128)(2,1)} %get-tuple-element.304), channel_id=1, source_target_pairs={{192,160},{224,128},{193,161},{225,129},{194,162},{226,130},{195,1... | collective-permute-start | bytes 786440 | tf_op jit(solution)/shard_map/ppermute | solution.py:249
  21.3 49.4 %collective-permute-start.8 = (bf16[128,1024]{1,0:T(8,128)(2,1)}, bf16[128,1024]{1,0:T(8,128)(2,1)}, u32[]{:S(2)}, u32[]{:S(2)}) collective-permute-start(bf16[128,1024]{1,0:T(8,128)(2,1)} %get-tuple-element.301), channel_id=1, source_target_pairs={{192,160},{224,128},{193,161},{225,129},{194,162},{226,130},{195,1... | collective-permute-start | bytes 786440 | tf_op jit(solution)/shard_map/ppermute | solution.py:249
  41.4 37.3 %collective-permute-start.9 = (bf16[2,128,1024]{2,1,0:T(8,128)(2,1)}, bf16[2,128,1024]{2,1,0:T(8,128)(2,1)}, u32[]{:S(2)}, u32[]{:S(2)}) collective-permute-start(bf16[2,128,1024]{2,1,0:T(8,128)(2,1)} %param.27), channel_id=1, source_target_pairs={{192,224},{224,192},{193,225},{225,193},{194,226},{226,194},{195,2... | collective-permute-start | bytes 1572872 | tf_op jit(solution)/shard_map/ppermute | solution.py:237
  60.1 11.9 %collective-permute-start.2 = (bf16[128,1024]{1,0:T(8,128)(2,1)}, bf16[128,1024]{1,0:T(8,128)(2,1)S(1)}, u32[]{:S(2)}, u32[]{:S(2)}) collective-permute-start(bf16[128,1024]{1,0:T(8,128)(2,1)} %get-tuple-element.303), channel_id=1, source_target_pairs={{64,0},{96,32},{65,1},{97,33},{66,2},{98,34},{67,3},{99,35},{68,4}... | collective-permute-start | bytes 786440 | tf_op jit(solution)/shard_map/ppermute | solution.py:249
  61.4 13.5 %collective-permute-start.5 = (bf16[128,1024]{1,0:T(8,128)(2,1)}, bf16[128,1024]{1,0:T(8,128)(2,1)S(1)}, u32[]{:S(2)}, u32[]{:S(2)}) collective-permute-start(bf16[128,1024]{1,0:T(8,128)(2,1)} %get-tuple-element.306), channel_id=1, source_target_pairs={{64,0},{96,32},{65,1},{97,33},{66,2},{98,34},{67,3},{99,35},{68,4}... | collective-permute-start | bytes 786440 | tf_op jit(solution)/shard_map/ppermute | solution.py:249
  62.8 6.5 %copy-start.11 = (bf16[128,1024]{1,0:T(8,128)(2,1)S(1)}, bf16[128,1024]{1,0:T(8,128)(2,1)}, u32[]{:S(2)}) copy-start(bf16[128,1024]{1,0:T(8,128)(2,1)} %get-tuple-element.303) | copy-start | bytes 786436
  62.8 7.9 %copy-start.13 = (bf16[128,1024]{1,0:T(8,128)(2,1)S(1)}, bf16[128,1024]{1,0:T(8,128)(2,1)}, u32[]{:S(2)}) copy-start(bf16[128,1024]{1,0:T(8,128)(2,1)} %get-tuple-element.306) | copy-start | bytes 786436
  62.8 14.5 %copy-start.8 = (bf16[2,128,1024]{2,1,0:T(8,128)(2,1)S(1)}, bf16[2,128,1024]{2,1,0:T(8,128)(2,1)}, u32[]{:S(2)}) copy-start(bf16[2,128,1024]{2,1,0:T(8,128)(2,1)} %param.27) | copy-start | bytes 1572868
  69.4 9.4 %collective-permute-start.6 = (bf16[128,1024]{1,0:T(8,128)(2,1)S(1)}, bf16[128,1024]{1,0:T(8,128)(2,1)S(1)}, u32[]{:S(2)}, u32[]{:S(2)}) collective-permute-start(bf16[128,1024]{1,0:T(8,128)(2,1)S(1)} %copy-done.11), channel_id=1, source_target_pairs={{64,32},{96,0},{65,33},{97,1},{66,34},{98,2},{67,35},{99,3},{68,36... | collective-permute-start | bytes 786440 | tf_op jit(solution)/shard_map/ppermute | solution.py:249
  70.7 10.2 %collective-permute-start.10 = (bf16[128,1024]{1,0:T(8,128)(2,1)S(1)}, bf16[128,1024]{1,0:T(8,128)(2,1)S(1)}, u32[]{:S(2)}, u32[]{:S(2)}) collective-permute-start(bf16[128,1024]{1,0:T(8,128)(2,1)S(1)} %copy-done.13), channel_id=1, source_target_pairs={{64,32},{96,0},{65,33},{97,1},{66,34},{98,2},{67,35},{99,3},{68,36... | collective-permute-start | bytes 786440 | tf_op jit(solution)/shard_map/ppermute | solution.py:249
  72.0 6.7 %copy-start.15 = (bf16[128,1024]{1,0:T(8,128)(2,1)}, bf16[128,1024]{1,0:T(8,128)(2,1)S(1)}, u32[]{:S(2)}) copy-start(bf16[128,1024]{1,0:T(8,128)(2,1)S(1)} %collective-permute-done.2) | copy-start | bytes 786436
  72.0 8.9 %collective-permute-start.7 = (bf16[128,1024]{1,0:T(8,128)(2,1)}, bf16[128,1024]{1,0:T(8,128)(2,1)S(1)}, u32[]{:S(2)}, u32[]{:S(2)}) collective-permute-start(bf16[128,1024]{1,0:T(8,128)(2,1)} %collective-permute-done.1), channel_id=1, source_target_pairs={{64,96},{96,64},{65,97},{97,65},{66,98},{98,66},{67,99},{99,67},{6... | collective-permute-start | bytes 786440 | tf_op jit(solution)/shard_map/ppermute | solution.py:261
  74.9 3.8 %copy-start.14 = (bf16[128,1024]{1,0:T(8,128)(2,1)}, bf16[128,1024]{1,0:T(8,128)(2,1)S(1)}, u32[]{:S(2)}) copy-start(bf16[128,1024]{1,0:T(8,128)(2,1)S(1)} %collective-permute-done.5) | copy-start | bytes 786436
  74.9 8.9 %collective-permute-start.11 = (bf16[128,1024]{1,0:T(8,128)(2,1)}, bf16[128,1024]{1,0:T(8,128)(2,1)S(1)}, u32[]{:S(2)}, u32[]{:S(2)}) collective-permute-start(bf16[128,1024]{1,0:T(8,128)(2,1)} %collective-permute-done.4), channel_id=1, source_target_pairs={{64,96},{96,64},{65,97},{97,65},{66,98},{98,66},{67,99},{99,67},{6... | collective-permute-start | bytes 786440 | tf_op jit(solution)/shard_map/ppermute | solution.py:261
  77.4 7.6 %copy-start.1 = (bf16[1,1024,1536]{2,1,0:T(8,128)(2,1)S(1)}, bf16[1,1024,1536]{2,1,0:T(8,128)(2,1)}, u32[]{:S(2)}) copy-start(bf16[1,1024,1536]{2,1,0:T(8,128)(2,1)} %param.26) | copy-start | bytes 9437188
  90.9 24.6 %collective-permute-start.16 = (bf16[3,2,128,768]{3,2,1,0:T(8,128)(2,1)}, bf16[3,2,128,768]{3,2,1,0:T(8,128)(2,1)S(1)}, u32[]{:S(2)}, u32[]{:S(2)}) collective-permute-start(bf16[3,2,128,768]{3,2,1,0:T(8,128)(2,1)} %get-tuple-element.268), channel_id=1, source_target_pairs={{0,24},{8,16},{16,8},{24,0},{1,25},{9,17},{17,9},{25,1},{2,26},{10... | collective-permute-start | bytes 3538952 | tf_op jit(solution)/shard_map/ppermute | solution.py:286
  99.3 16.2 %copy-start.10 = (bf16[3,2,128,768]{3,2,1,0:T(8,128)(2,1)S(1)}, bf16[3,2,128,768]{3,2,1,0:T(8,128)(2,1)}, u32[]{:S(2)}) copy-start(bf16[3,2,128,768]{3,2,1,0:T(8,128)(2,1)} %get-tuple-element.267) | copy-start | bytes 3538948
  100.7 28.3 %collective-permute-start.14 = (bf16[3,2,128,768]{3,2,0,1:T(8,128)(2,1)S(1)}, bf16[3,2,128,768]{3,2,0,1:T(8,128)(2,1)S(1)}, u32[]{:S(2)}, u32[]{:S(2)}) collective-permute-start(bf16[3,2,128,768]{3,2,0,1:T(8,128)(2,1)S(1)} %copy.11), channel_id=1, source_target_pairs={{0,8},{8,0},{16,24},{24,16},{1,9},{9,1},{17,25},{25,17},{2,10},{10... | collective-permute-start | bytes 3538952 | tf_op jit(solution)/shard_map/ppermute | solution.py:286
  115.9 13.1 %copy-start.9 = (bf16[3,2,128,768]{3,2,1,0:T(8,128)(2,1)S(1)}, bf16[3,2,128,768]{3,2,1,0:T(8,128)(2,1)}, u32[]{:S(2)}) copy-start(bf16[3,2,128,768]{3,2,1,0:T(8,128)(2,1)} %get-tuple-element.265) | copy-start | bytes 3538948
  115.9 21.2 %collective-permute-start.17 = (bf16[3,128,768]{2,1,0:T(8,128)(2,1)S(1)}, bf16[3,128,768]{2,1,0:T(8,128)(2,1)S(1)}, u32[]{:S(2)}, u32[]{:S(2)}) collective-permute-start(bf16[3,128,768]{2,1,0:T(8,128)(2,1)S(1)} %slice_bitcast_fusion), channel_id=1, source_target_pairs={{0,8},{8,0},{16,24},{24,16},{1,9},{9,1},{17,25},{25,17},{2,10},{10... | collective-permute-start | bytes 1769480 | tf_op jit(solution)/shard_map/ppermute | solution.py:287
  129.2 10.0 %collective-permute-start.15 = (bf16[3,128,768]{2,1,0:T(8,128)(2,1)S(1)}, bf16[3,128,768]{2,1,0:T(8,128)(2,1)S(1)}, u32[]{:S(2)}, u32[]{:S(2)}) collective-permute-start(bf16[3,128,768]{2,1,0:T(8,128)(2,1)S(1)} %slice_bitcast_fusion.2), channel_id=1, source_target_pairs={{0,24},{8,16},{16,8},{24,0},{1,25},{9,17},{17,9},{25,1},{2,26},{10... | collective-permute-start | bytes 1769480 | tf_op jit(solution)/shard_map/ppermute | solution.py:287
  137.2 2.9 %copy-start.5 = (bf16[1,3,128,768]{3,2,1,0:T(8,128)(2,1)}, bf16[1,3,128,768]{3,2,1,0:T(8,128)(2,1)S(1)}, u32[]{:S(2)}) copy-start(bf16[1,3,128,768]{3,2,1,0:T(8,128)(2,1)S(1)} %fusion.1) | copy-start | bytes 1769476
  139.2 23.5 %copy-start = (bf16[1,1024,1536]{2,1,0:T(8,128)(2,1)S(1)}, bf16[1,1024,1536]{2,1,0:T(8,128)(2,1)}, u32[]{:S(2)}) copy-start(bf16[1,1024,1536]{2,1,0:T(8,128)(2,1)} %param.24) | copy-start | bytes 9437188
  139.3 1.1 copy-start.7
  139.3 23.4 %copy-start.12 = (bf16[128,1024]{1,0:T(8,128)(2,1)S(1)}, bf16[128,1024]{1,0:T(8,128)(2,1)}, u32[]{:S(2)}) copy-start(bf16[128,1024]{1,0:T(8,128)(2,1)} %get-tuple-element.303) | copy-start | bytes 786436
  140.3 13.3 %collective-permute-start.18 = (bf16[2,3,16,768]{3,2,1,0:T(8,128)(2,1)S(1)}, bf16[2,3,16,768]{3,2,1,0:T(8,128)(2,1)}, u32[]{:S(2)}, u32[]{:S(2)}) collective-permute-start(bf16[2,3,16,768]{3,2,1,0:T(8,128)(2,1)S(1)} %get-tuple-element.275), channel_id=1, source_target_pairs={{0,1},{1,2},{2,3},{3,4},{4,5},{5,6},{6,7},{7,0},{8,9},{9,10},{10,1... | collective-permute-start | bytes 442376 | tf_op jit(solution)/shard_map/ppermute | solution.py:294
  141.9 20.7 %collective-permute-start.19 = (bf16[2,3,16,768]{3,2,1,0:T(8,128)(2,1)S(1)}, bf16[2,3,16,768]{3,2,1,0:T(8,128)(2,1)}, u32[]{:S(2)}, u32[]{:S(2)}) collective-permute-start(bf16[2,3,16,768]{3,2,1,0:T(8,128)(2,1)S(1)} %get-tuple-element.276), channel_id=1, source_target_pairs={{0,2},{1,3},{2,4},{3,5},{4,6},{5,7},{6,0},{7,1},{8,10},{9,11},{10,... | collective-permute-start | bytes 442376 | tf_op jit(solution)/shard_map/ppermute | solution.py:294
  144.9 22.2 %collective-permute-start.20 = (bf16[2,3,16,768]{3,2,1,0:T(8,128)(2,1)}, bf16[2,3,16,768]{3,2,1,0:T(8,128)(2,1)}, u32[]{:S(2)}, u32[]{:S(2)}) collective-permute-start(bf16[2,3,16,768]{3,2,1,0:T(8,128)(2,1)} %get-tuple-element.277), channel_id=1, source_target_pairs={{0,3},{1,4},{2,5},{3,6},{4,7},{5,0},{6,1},{7,2},{8,11},{9,12},{10,... | collective-permute-start | bytes 442376 | tf_op jit(solution)/shard_map/ppermute | solution.py:294
  148.7 18.4 %collective-permute-start.21 = (bf16[2,3,16,768]{3,2,1,0:T(8,128)(2,1)}, bf16[2,3,16,768]{3,2,1,0:T(8,128)(2,1)}, u32[]{:S(2)}, u32[]{:S(2)}) collective-permute-start(bf16[2,3,16,768]{3,2,1,0:T(8,128)(2,1)} %get-tuple-element.278), channel_id=1, source_target_pairs={{0,4},{1,5},{2,6},{3,7},{4,0},{5,1},{6,2},{7,3},{8,12},{9,13},{10,... | collective-permute-start | bytes 442376 | tf_op jit(solution)/shard_map/ppermute | solution.py:294
  149.2 21.0 %collective-permute-start.22 = (bf16[2,3,16,768]{3,2,1,0:T(8,128)(2,1)}, bf16[2,3,16,768]{3,2,1,0:T(8,128)(2,1)}, u32[]{:S(2)}, u32[]{:S(2)}) collective-permute-start(bf16[2,3,16,768]{3,2,1,0:T(8,128)(2,1)} %get-tuple-element.279), channel_id=1, source_target_pairs={{0,5},{1,6},{2,7},{3,0},{4,1},{5,2},{6,3},{7,4},{8,13},{9,14},{10,... | collective-permute-start | bytes 442376 | tf_op jit(solution)/shard_map/ppermute | solution.py:294
  153.6 18.4 %collective-permute-start.23 = (bf16[2,3,16,768]{3,2,1,0:T(8,128)(2,1)}, bf16[2,3,16,768]{3,2,1,0:T(8,128)(2,1)}, u32[]{:S(2)}, u32[]{:S(2)}) collective-permute-start(bf16[2,3,16,768]{3,2,1,0:T(8,128)(2,1)} %get-tuple-element.281), channel_id=1, source_target_pairs={{0,6},{1,7},{2,0},{3,1},{4,2},{5,3},{6,4},{7,5},{8,14},{9,15},{10,... | collective-permute-start | bytes 442376 | tf_op jit(solution)/shard_map/ppermute | solution.py:294
  162.7 11.9 %collective-permute-start.24 = (bf16[2,3,16,768]{3,2,1,0:T(8,128)(2,1)}, bf16[2,3,16,768]{3,2,1,0:T(8,128)(2,1)}, u32[]{:S(2)}, u32[]{:S(2)}) collective-permute-start(bf16[2,3,16,768]{3,2,1,0:T(8,128)(2,1)} %get-tuple-element.280), channel_id=1, source_target_pairs={{0,7},{1,0},{2,1},{3,2},{4,3},{5,4},{6,5},{7,6},{8,15},{9,8},{10,9... | collective-permute-start | bytes 442376 | tf_op jit(solution)/shard_map/ppermute | solution.py:294
  162.7 11.8 %copy-start.6 = (bf16[1,3,128,768]{3,2,1,0:T(8,128)(2,1)S(1)}, bf16[1,3,128,768]{3,2,1,0:T(8,128)(2,1)}, u32[]{:S(2)}) copy-start(bf16[1,3,128,768]{3,2,1,0:T(8,128)(2,1)} %copy-done.5) | copy-start | bytes 1769476
